TPU v7x, 512 devices: a whole 4x4x16 slice. The times are simulated.
512 devices in a mesh: mem: 128 (over x, y, z_lo), slab: 4 (over z_hi, core).
Axes of the slice: x: 4, y: 4, z: 16 (z_hi: 2, z_lo: 8; z = z_hi * 8 + z_lo), core: 2. Of those that a mesh axis runs over, the one named last changes fastest.
Arguments:
- prior_sample_stack: float32 [128, 3, 256, 512], P('mem', None, None, 'slab'), may hold values from -4 to 4
- obs_cell: int32 [128, 512], P('mem', 'slab'), may hold values from 0 to 255
- obs_value: float32 [128, 512], P('mem', 'slab'), may hold values from -4 to 4
- obs_bin: int32 [128, 512], P('mem', 'slab'), may hold values from 0 to 3
Outputs:
- analysis: float32 [128, 3, 256, 512], P('mem', None, None, 'slab')
Inputs may be any that keep to these rules, and one draw needn't show every extreme that they name: obs_cell is local row times 128 plus local column within the observation's region rows and its index of slab's columns.
All inputs are finite; a program needn't handle non-finite values.
Results may differ from a plain program's by a relative error of at most 0.0003.
Values sent between devices are 32-bit elements; how exact they have to be, the bound alone decides.
A program may use at most 64 MiB of HBM per device.

v0:
```python
import math
import jax
import jax.numpy as jnp
from jax import lax
from jax.sharding import PartitionSpec as P

STEPS = 12
SWEEPS = 8
time_step = 0.25
gravity = 1.0
mean_depth = 1.0
coriolis = 0.2
viscosity = 0.4
inflation = 1.1
highest = lax.Precision.HIGHEST


def padded_2(cells, sides, width):
    for axis, dim in sides:
        count = lax.axis_size(axis)
        head = lax.slice_in_dim(cells, 0, width, axis=dim)
        tail = lax.slice_in_dim(cells, cells.shape[dim] - width, cells.shape[dim], axis=dim)
        cells = jnp.concatenate(
            [
                lax.ppermute(tail, axis, [(i, (i + 1) % count) for i in range(count)]),
                cells,
                lax.ppermute(head, axis, [((i + 1) % count, i) for i in range(count)]),
            ],
            axis=dim,
        )
    return cells


def passed_along(value, axis, steps):
    count = lax.axis_size(axis)
    pairs = [(source, (source + steps) % count) for source in range(count)]
    return lax.ppermute(value, axis, pairs)


def sent_to_all(value, axis):
    size = lax.axis_size(axis)
    return lax.all_to_all(
        jnp.broadcast_to(value[None], (size, *value.shape)), axis, 0, 0, tiled=True
    )


def over_copies(value, axis):
    return sent_to_all(value, axis).sum(axis=0)


def together(arrays, axis):
    ends = [0]
    for a in arrays:
        ends.append(ends[-1] + a.size)
    running = over_copies(jnp.concatenate([a.ravel() for a in arrays]), axis)
    return tuple((running[b:e].reshape(a.shape) for a, b, e in zip(arrays, ends, ends[1:])))


def centre(values):
    return values[:, 1:-1]


def east_of(values):
    return jnp.roll(values[:, 1:-1], -1, 0)


def west_of(values):
    return jnp.roll(values[:, 1:-1], 1, 0)


def north_of(values):
    return values[:, 2:]


def south_of(values):
    return values[:, :-2]


def spread(values):
    return (
        east_of(values)
        + west_of(values)
        + north_of(values)
        + south_of(values)
        - 4.0 * centre(values)
    )


def slope_x(values):
    return 0.5 * (east_of(values) - west_of(values))


def slope_y(values):
    return 0.5 * (north_of(values) - south_of(values))


def advance(padded):
    elevation_anomaly = padded[0]
    east_wind = padded[1]
    north_wind = padded[2]
    flux_x = (mean_depth + elevation_anomaly) * east_wind
    flux_y = (mean_depth + elevation_anomaly) * north_wind
    east_mid = centre(east_wind)
    north_mid = centre(north_wind)
    new_height = centre(elevation_anomaly) + time_step * (
        viscosity * spread(elevation_anomaly) - slope_x(flux_x) - slope_y(flux_y)
    )
    new_east = east_mid + time_step * (
        viscosity * spread(east_wind)
        - east_mid * slope_x(east_wind)
        - north_mid * slope_y(east_wind)
        - gravity * slope_x(elevation_anomaly)
        + coriolis * north_mid
    )
    new_north = north_mid + time_step * (
        viscosity * spread(north_wind)
        - east_mid * slope_x(north_wind)
        - north_mid * slope_y(north_wind)
        - gravity * slope_y(elevation_anomaly)
        - coriolis * east_mid
    )
    return jnp.stack([new_height, new_east, new_north])


def partial_sums(anomaly, distance, obs_weight, innovation, band_rows):
    target = jnp.arange(band_rows).astype(jnp.float32)
    scaled_dist = (distance[None, :] - target[:, None]) / float(band_rows)
    weight = obs_weight[None, :] * jnp.exp(-0.5 * scaled_dist * scaled_dist)
    scaled = anomaly[None, :, :] * weight[:, None, :]
    gram_matrix = jnp.einsum("tmj,kj->tmk", scaled, anomaly, precision=highest)
    pull_vector = jnp.einsum("tmj,j->tm", scaled, innovation, precision=highest)
    return (gram_matrix, pull_vector)


def batch_product(left, right):
    return jnp.einsum("tij,tjk->tik", left, right, precision=highest)


def weights_from(gram_matrix, pull_vector, members):
    identity = jnp.eye(members, dtype=jnp.float32)
    gram_matrix = gram_matrix + (members - 1) / inflation * identity[None]
    traces = jnp.trace(gram_matrix, axis1=1, axis2=2)
    iterate = gram_matrix / traces[:, None, None]
    inverse = jnp.broadcast_to(identity, gram_matrix.shape)
    for iteration in range(SWEEPS):
        correction = 1.5 * identity[None] - 0.5 * batch_product(inverse, iterate)
        iterate, inverse = (batch_product(iterate, correction), batch_product(correction, inverse))
    inv_root = inverse / jnp.sqrt(traces)[:, None, None]
    inner = jnp.einsum("tij,tj->ti", inv_root, pull_vector, precision=highest)
    mean_weights = jnp.einsum("tij,tj->ti", inv_root, inner, precision=highest)
    return math.sqrt(members - 1) * inv_root + mean_weights[:, :, None]


def apply_weights(zone_portion, mixing):
    mean_state = jnp.mean(zone_portion, axis=0)
    spread_state = zone_portion - mean_state[None]
    return mean_state[None] + jnp.einsum("mftc,tmk->kftc", spread_state, mixing, precision=highest)


def local(prior_sample_stack, obs_cell, obs_value, obs_bin):
    current_condition = prior_sample_stack[0]

    def four_steps(counter, values):
        padded = padded_2(values, (("slab", 2),), 4)
        for substep in range(4):
            padded = advance(padded)
        return padded

    current_condition = lax.fori_loop(0, STEPS // 4, four_steps, current_condition)
    predicted_grid = current_condition[None]
    zone_collection = lax.all_to_all(predicted_grid, "mem", split_axis=2, concat_axis=0, tiled=True)
    heights = zone_collection[:, 0]
    members = heights.shape[0]
    band_rows = heights.shape[1]
    columns = heights.shape[2]
    observed = jnp.take(heights.reshape(members, band_rows * columns), obs_cell[0], axis=1)
    obs_mean = jnp.mean(observed, axis=0)
    anomaly = observed - obs_mean[None]
    extras = jnp.stack(
        [
            obs_value[0] - obs_mean,
            10.0 / (1.0 + obs_bin[0].astype(jnp.float32)),
            (obs_cell[0] // columns).astype(jnp.float32),
        ]
    )
    package = (anomaly, extras)
    collected = [(0, package)]
    for stride in (1, -1, 2, -2):
        collected.append((-stride, passed_along((package[0], package[1]), "mem", stride)))
    all_anomaly = jnp.concatenate([entry[1][0] for entry in collected], axis=1)
    distance = jnp.concatenate(
        [entry[1][1][2] + float(entry[0] * band_rows) for entry in collected]
    )
    obs_weight = jnp.concatenate([entry[1][1][1] for entry in collected])
    innovation = jnp.concatenate([entry[1][1][0] for entry in collected])
    gram_matrix, pull_vector = partial_sums(
        all_anomaly, distance, obs_weight, innovation, band_rows
    )
    gram_matrix, pull_vector = together((gram_matrix, pull_vector), "slab")
    mixing = weights_from(gram_matrix, pull_vector, members)
    return lax.all_to_all(
        apply_weights(zone_collection, mixing), "mem", split_axis=0, concat_axis=2, tiled=True
    )


def solution(mesh):
    placed = (P("mem", None, None, "slab"), P("mem", "slab"), P("mem", "slab"), P("mem", "slab"))
    return jax.shard_map(
        local, mesh=mesh, in_specs=placed, out_specs=P("mem", None, None, "slab"), check_vma=False
    )
```

profile of v0, /device:TPU:1, one launch (start us, length us, event | category | flops | bytes accessed | tf_op | source)
XLA Modules:
  0.0 343.0 jit_solution(7744454603862353869)
XLA Ops:
  0.0 1.0 copy-done
  1.0 111.7 %while.10 = (s32[]{:T(128)}, f32[3,256,128]{2,1,0:T(8,128)S(1)}, s32[]{:T(128)}) while((s32[]{:T(128)}, f32[3,256,128]{2,1,0:T(8,128)S(1)}, s32[]{:T(128)}) %tuple.159), condition=%wide.region_1.2_spmd, body=%wide.region_0.1_spmd.sunk | while | flops 9566210 | bytes 27316348 | solution.py:169
  1.2 8.7 %collective-permute-start = (f32[3,256,4]{2,1,0:T(8,128)S(1)}, f32[3,256,4]{2,1,0:T(8,128)S(1)}, u32[]{:S(2)}, u32[]{:S(2)}) collective-permute-start(f32[3,256,4]{2,1,0:T(8,128)S(1)} %get-tuple-element.233), channel_id=1, source_target_pairs={{1,0},{2,1},{3,2},{0,3},{5,4},{6,5},{7,6},{4,7},{9,8},{10,9},{11,1... | collective-permute-start | bytes 36872 | tf_op jit(solution)/shard_map/while/body/eval_jaxpr/ppermute | solution.py:27
  9.9 10.0 %collective-permute-start.1 = (f32[3,256,4]{2,1,0:T(8,128)S(1)}, f32[3,256,4]{2,1,0:T(8,128)S(1)}, u32[]{:S(2)}, u32[]{:S(2)}) collective-permute-start(f32[3,256,4]{2,1,0:T(8,128)S(1)} %get-tuple-element.234), channel_id=1, source_target_pairs={{0,1},{1,2},{2,3},{3,0},{4,5},{5,6},{6,7},{7,4},{8,9},{9,10},{10,1... | collective-permute-start | bytes 36872 | tf_op jit(solution)/shard_map/while/body/eval_jaxpr/ppermute | solution.py:25
  19.9 3.8 %collective-permute-done = f32[3,256,4]{2,1,0:T(8,128)S(1)} collective-permute-done((f32[3,256,4]{2,1,0:T(8,128)S(1)}, f32[3,256,4]{2,1,0:T(8,128)S(1)}, u32[]{:S(2)}, u32[]{:S(2)}) %collective-permute-start) | collective-permute-done | bytes 12320 | tf_op jit(solution)/shard_map/while/body/eval_jaxpr/ppermute | solution.py:27
  23.7 18.3 %collective-permute-done.1 = f32[3,256,4]{2,1,0:T(8,128)S(1)} collective-permute-done((f32[3,256,4]{2,1,0:T(8,128)S(1)}, f32[3,256,4]{2,1,0:T(8,128)S(1)}, u32[]{:S(2)}, u32[]{:S(2)}) %collective-permute-start.1) | collective-permute-done | bytes 12320 | tf_op jit(solution)/shard_map/while/body/eval_jaxpr/ppermute | solution.py:25
  42.0 0.4 pad_maximum_fusion.30
  42.5 0.3 fusion.192
  43.0 0.3 fusion.190
  43.4 0.6 add_multiply_fusion.16
  44.8 0.3 add_multiply_fusion.17
  45.4 0.6 add_multiply_fusion.18
  46.8 0.3 add_multiply_fusion.19
  47.5 0.6 add_multiply_fusion.20
  48.7 0.3 add_multiply_fusion.21
  50.1 3.3 collective-permute-start
  53.4 11.9 %collective-permute-start.1 = (f32[3,256,4]{2,1,0:T(8,128)S(1)}, f32[3,256,4]{2,1,0:T(8,128)S(1)}, u32[]{:S(2)}, u32[]{:S(2)}) collective-permute-start(f32[3,256,4]{2,1,0:T(8,128)S(1)} %get-tuple-element.234), channel_id=1, source_target_pairs={{0,1},{1,2},{2,3},{3,0},{4,5},{5,6},{6,7},{7,4},{8,9},{9,10},{10,1... | collective-permute-start | bytes 36872 | tf_op jit(solution)/shard_map/while/body/eval_jaxpr/ppermute | solution.py:25
  65.4 11.8 %collective-permute-done = f32[3,256,4]{2,1,0:T(8,128)S(1)} collective-permute-done((f32[3,256,4]{2,1,0:T(8,128)S(1)}, f32[3,256,4]{2,1,0:T(8,128)S(1)}, u32[]{:S(2)}, u32[]{:S(2)}) %collective-permute-start) | collective-permute-done | bytes 12320 | tf_op jit(solution)/shard_map/while/body/eval_jaxpr/ppermute | solution.py:27
  77.1 0.4 pad_maximum_fusion.30
  77.6 0.3 fusion.192
  78.1 0.3 fusion.190
  78.5 0.6 add_multiply_fusion.16
  79.9 0.3 add_multiply_fusion.17
  80.5 0.6 add_multiply_fusion.18
  81.9 0.3 add_multiply_fusion.19
  82.6 0.6 add_multiply_fusion.20
  83.8 0.3 add_multiply_fusion.21
  85.2 5.1 %collective-permute-start = (f32[3,256,4]{2,1,0:T(8,128)S(1)}, f32[3,256,4]{2,1,0:T(8,128)S(1)}, u32[]{:S(2)}, u32[]{:S(2)}) collective-permute-start(f32[3,256,4]{2,1,0:T(8,128)S(1)} %get-tuple-element.233), channel_id=1, source_target_pairs={{1,0},{2,1},{3,2},{0,3},{5,4},{6,5},{7,6},{4,7},{9,8},{10,9},{11,1... | collective-permute-start | bytes 36872 | tf_op jit(solution)/shard_map/while/body/eval_jaxpr/ppermute | solution.py:27
  90.3 9.4 %collective-permute-start.1 = (f32[3,256,4]{2,1,0:T(8,128)S(1)}, f32[3,256,4]{2,1,0:T(8,128)S(1)}, u32[]{:S(2)}, u32[]{:S(2)}) collective-permute-start(f32[3,256,4]{2,1,0:T(8,128)S(1)} %get-tuple-element.234), channel_id=1, source_target_pairs={{0,1},{1,2},{2,3},{3,0},{4,5},{5,6},{6,7},{7,4},{8,9},{9,10},{10,1... | collective-permute-start | bytes 36872 | tf_op jit(solution)/shard_map/while/body/eval_jaxpr/ppermute | solution.py:25
  99.7 5.1 %collective-permute-done = f32[3,256,4]{2,1,0:T(8,128)S(1)} collective-permute-done((f32[3,256,4]{2,1,0:T(8,128)S(1)}, f32[3,256,4]{2,1,0:T(8,128)S(1)}, u32[]{:S(2)}, u32[]{:S(2)}) %collective-permute-start) | collective-permute-done | bytes 12320 | tf_op jit(solution)/shard_map/while/body/eval_jaxpr/ppermute | solution.py:27
  104.8 0.4 pad_maximum_fusion.30
  105.4 0.3 fusion.192
  106.2 0.6 add_multiply_fusion.16
  107.6 0.3 add_multiply_fusion.17
  108.2 0.6 add_multiply_fusion.18
  109.7 0.3 add_multiply_fusion.19
  110.3 0.6 add_multiply_fusion.20
  111.5 0.3 add_multiply_fusion.21
  112.7 1.2 copy.44
  113.9 47.4 %all-to-all-start = ((f32[1,3,256,128]{3,0,1,2:T(1,128)}), f32[1,3,256,128]{3,0,1,2:T(1,128)S(1)}, u32[]{:S(2)}, u32[]{:S(2)}) async-start(f32[1,3,256,128]{3,0,1,2:T(1,128)} %copy.44), calls=%async_computation | async-start | bytes 786432 | tf_op jit(solution)/shard_map/all_to_all | solution.py:171
  161.3 0.6 copy-done.3
  162.0 0.6 copy-done.4
  162.6 23.9 %all-to-all-done = f32[1,3,256,128]{3,0,1,2:T(1,128)S(1)} async-done(((f32[1,3,256,128]{3,0,1,2:T(1,128)}), f32[1,3,256,128]{3,0,1,2:T(1,128)S(1)}, u32[]{:S(2)}, u32[]{:S(2)}) %all-to-all-start) | async-done | bytes 393248 | tf_op jit(solution)/shard_map/all_to_all | solution.py:171
  186.7 0.6 gather_fusion
  187.5 0.6 copy-done.2
  188.2 2.6 collective-permute-start.6
  190.8 13.5 %collective-permute-start.7 = (f32[3,128]{1,0:T(4,128)S(1)}, f32[3,128]{1,0:T(4,128)S(1)}, u32[]{:S(2)}, u32[]{:S(2)}) collective-permute-start(f32[3,128]{1,0:T(4,128)S(1)} %pad_maximum_fusion.27), channel_id=1, source_target_pairs={{0,508},{4,0},{8,4},{12,8},{16,12},{20,16},{24,20},{28,24},{32,28}... | collective-permute-start | bytes 4616 | tf_op jit(solution)/shard_map/ppermute | solution.py:37
  204.3 1.9 collective-permute-start.8
  206.2 13.3 %collective-permute-start.9 = (f32[3,128]{1,0:T(4,128)S(1)}, f32[3,128]{1,0:T(4,128)S(1)}, u32[]{:S(2)}, u32[]{:S(2)}) collective-permute-start(f32[3,128]{1,0:T(4,128)S(1)} %pad_maximum_fusion.27), channel_id=1, source_target_pairs={{0,504},{4,508},{8,0},{12,4},{16,8},{20,12},{24,16},{28,20},{32,24... | collective-permute-start | bytes 4616 | tf_op jit(solution)/shard_map/ppermute | solution.py:37
  219.5 1.9 collective-permute-start.2
  221.5 14.2 %collective-permute-start.3 = (f32[128,128]{1,0:T(8,128)S(1)}, f32[128,128]{1,0:T(8,128)S(1)}, u32[]{:S(2)}, u32[]{:S(2)}) collective-permute-start(f32[128,128]{1,0:T(8,128)S(1)} %get-tuple-element.38), channel_id=1, source_target_pairs={{0,508},{4,0},{8,4},{12,8},{16,12},{20,16},{24,20},{28,24},{32,28}... | collective-permute-start | bytes 196616 | tf_op jit(solution)/shard_map/ppermute | solution.py:37
  235.7 1.9 collective-permute-start.4
  237.7 13.3 %collective-permute-start.5 = (f32[128,128]{1,0:T(8,128)S(1)}, f32[128,128]{1,0:T(8,128)S(1)}, u32[]{:S(2)}, u32[]{:S(2)}) collective-permute-start(f32[128,128]{1,0:T(8,128)S(1)} %get-tuple-element.38), channel_id=1, source_target_pairs={{0,504},{4,508},{8,0},{12,4},{16,8},{20,12},{24,16},{28,20},{32,24... | collective-permute-start | bytes 196616 | tf_op jit(solution)/shard_map/ppermute | solution.py:37
  251.2 1.1 collective-permute-done.5
  252.3 0.7 fusion.36
  253.0 0.6 fusion.34
  253.7 1.1 broadcast_in_dim.31
  254.8 20.6 %all-to-all-start.1 = ((f32[4,1,33024]{2,1,0:T(1,128)}), f32[4,1,33024]{2,1,0:T(1,128)S(1)}, u32[]{:S(2)}, u32[]{:S(2)}) async-start(f32[4,1,33024]{2,1,0:T(1,128)} %broadcast_in_dim.31), calls=%async_computation.1 | async-start | bytes 1056768 | tf_op jit(solution)/shard_map/all_to_all | solution.py:42
  275.4 16.5 %all-to-all-done.1 = f32[4,1,33024]{2,1,0:T(1,128)S(1)} async-done(((f32[4,1,33024]{2,1,0:T(1,128)}), f32[4,1,33024]{2,1,0:T(1,128)S(1)}, u32[]{:S(2)}, u32[]{:S(2)}) %all-to-all-start.1) | async-done | bytes 528416 | tf_op jit(solution)/shard_map/all_to_all | solution.py:42
  291.9 0.5 reduce_sum.39
  299.1 0.7 slice-done
  300.4 0.6 fusion.25
  301.3 40.8 %all_to_all.42 = f32[128,3,2,128]{3,2,1,0:T(2,128)S(1)} all-to-all(f32[128,3,2,128]{3,2,1,0:T(2,128)S(1)} %copy.51), channel_id=1, replica_groups=mesh['mem'=128,'slab'=4] {'mem'}, dimensions={0} | all-to-all | bytes 786432 | tf_op jit(solution)/shard_map/all_to_all | solution.py:201
  342.1 0.9 copy.52
  (182 shorter events, 20.6 us)
Async XLA Ops:
  0.0 1.0 copy-start
  1.2 22.6 %collective-permute-start = (f32[3,256,4]{2,1,0:T(8,128)S(1)}, f32[3,256,4]{2,1,0:T(8,128)S(1)}, u32[]{:S(2)}, u32[]{:S(2)}) collective-permute-start(f32[3,256,4]{2,1,0:T(8,128)S(1)} %get-tuple-element.233), channel_id=1, source_target_pairs={{1,0},{2,1},{3,2},{0,3},{5,4},{6,5},{7,6},{4,7},{9,8},{10,9},{11,1... | collective-permute-start | bytes 36872 | tf_op jit(solution)/shard_map/while/body/eval_jaxpr/ppermute | solution.py:27
  9.9 32.1 %collective-permute-start.1 = (f32[3,256,4]{2,1,0:T(8,128)S(1)}, f32[3,256,4]{2,1,0:T(8,128)S(1)}, u32[]{:S(2)}, u32[]{:S(2)}) collective-permute-start(f32[3,256,4]{2,1,0:T(8,128)S(1)} %get-tuple-element.234), channel_id=1, source_target_pairs={{0,1},{1,2},{2,3},{3,0},{4,5},{5,6},{6,7},{7,4},{8,9},{9,10},{10,1... | collective-permute-start | bytes 36872 | tf_op jit(solution)/shard_map/while/body/eval_jaxpr/ppermute | solution.py:25
  50.1 27.0 %collective-permute-start = (f32[3,256,4]{2,1,0:T(8,128)S(1)}, f32[3,256,4]{2,1,0:T(8,128)S(1)}, u32[]{:S(2)}, u32[]{:S(2)}) collective-permute-start(f32[3,256,4]{2,1,0:T(8,128)S(1)} %get-tuple-element.233), channel_id=1, source_target_pairs={{1,0},{2,1},{3,2},{0,3},{5,4},{6,5},{7,6},{4,7},{9,8},{10,9},{11,1... | collective-permute-start | bytes 36872 | tf_op jit(solution)/shard_map/while/body/eval_jaxpr/ppermute | solution.py:27
  53.4 23.7 %collective-permute-start.1 = (f32[3,256,4]{2,1,0:T(8,128)S(1)}, f32[3,256,4]{2,1,0:T(8,128)S(1)}, u32[]{:S(2)}, u32[]{:S(2)}) collective-permute-start(f32[3,256,4]{2,1,0:T(8,128)S(1)} %get-tuple-element.234), channel_id=1, source_target_pairs={{0,1},{1,2},{2,3},{3,0},{4,5},{5,6},{6,7},{7,4},{8,9},{9,10},{10,1... | collective-permute-start | bytes 36872 | tf_op jit(solution)/shard_map/while/body/eval_jaxpr/ppermute | solution.py:25
  85.2 19.6 %collective-permute-start = (f32[3,256,4]{2,1,0:T(8,128)S(1)}, f32[3,256,4]{2,1,0:T(8,128)S(1)}, u32[]{:S(2)}, u32[]{:S(2)}) collective-permute-start(f32[3,256,4]{2,1,0:T(8,128)S(1)} %get-tuple-element.233), channel_id=1, source_target_pairs={{1,0},{2,1},{3,2},{0,3},{5,4},{6,5},{7,6},{4,7},{9,8},{10,9},{11,1... | collective-permute-start | bytes 36872 | tf_op jit(solution)/shard_map/while/body/eval_jaxpr/ppermute | solution.py:27
  90.3 14.5 %collective-permute-start.1 = (f32[3,256,4]{2,1,0:T(8,128)S(1)}, f32[3,256,4]{2,1,0:T(8,128)S(1)}, u32[]{:S(2)}, u32[]{:S(2)}) collective-permute-start(f32[3,256,4]{2,1,0:T(8,128)S(1)} %get-tuple-element.234), channel_id=1, source_target_pairs={{0,1},{1,2},{2,3},{3,0},{4,5},{5,6},{6,7},{7,4},{8,9},{9,10},{10,1... | collective-permute-start | bytes 36872 | tf_op jit(solution)/shard_map/while/body/eval_jaxpr/ppermute | solution.py:25
  113.9 72.7 %all-to-all-start = ((f32[1,3,256,128]{3,0,1,2:T(1,128)}), f32[1,3,256,128]{3,0,1,2:T(1,128)S(1)}, u32[]{:S(2)}, u32[]{:S(2)}) async-start(f32[1,3,256,128]{3,0,1,2:T(1,128)} %copy.44), calls=%async_computation | async-start | bytes 786432 | tf_op jit(solution)/shard_map/all_to_all | solution.py:171
  161.3 0.7 copy-start.3
  162.0 0.7 copy-start.4
  187.5 0.7 copy-start.2
  188.2 33.3 %collective-permute-start.6 = (f32[3,128]{1,0:T(4,128)S(1)}, f32[3,128]{1,0:T(4,128)S(1)}, u32[]{:S(2)}, u32[]{:S(2)}) collective-permute-start(f32[3,128]{1,0:T(4,128)S(1)} %pad_maximum_fusion.27), channel_id=1, source_target_pairs={{0,4},{4,8},{8,12},{12,16},{16,20},{20,24},{24,28},{28,32},{32,36}... | collective-permute-start | bytes 4616 | tf_op jit(solution)/shard_map/ppermute | solution.py:37
  190.8 44.9 %collective-permute-start.7 = (f32[3,128]{1,0:T(4,128)S(1)}, f32[3,128]{1,0:T(4,128)S(1)}, u32[]{:S(2)}, u32[]{:S(2)}) collective-permute-start(f32[3,128]{1,0:T(4,128)S(1)} %pad_maximum_fusion.27), channel_id=1, source_target_pairs={{0,508},{4,0},{8,4},{12,8},{16,12},{20,16},{24,20},{28,24},{32,28}... | collective-permute-start | bytes 4616 | tf_op jit(solution)/shard_map/ppermute | solution.py:37
  204.3 33.4 %collective-permute-start.8 = (f32[3,128]{1,0:T(4,128)S(1)}, f32[3,128]{1,0:T(4,128)S(1)}, u32[]{:S(2)}, u32[]{:S(2)}) collective-permute-start(f32[3,128]{1,0:T(4,128)S(1)} %pad_maximum_fusion.27), channel_id=1, source_target_pairs={{0,8},{4,12},{8,16},{12,20},{16,24},{20,28},{24,32},{28,36},{32,40... | collective-permute-start | bytes 4616 | tf_op jit(solution)/shard_map/ppermute | solution.py:37
  206.2 44.8 %collective-permute-start.9 = (f32[3,128]{1,0:T(4,128)S(1)}, f32[3,128]{1,0:T(4,128)S(1)}, u32[]{:S(2)}, u32[]{:S(2)}) collective-permute-start(f32[3,128]{1,0:T(4,128)S(1)} %pad_maximum_fusion.27), channel_id=1, source_target_pairs={{0,504},{4,508},{8,0},{12,4},{16,8},{20,12},{24,16},{28,20},{32,24... | collective-permute-start | bytes 4616 | tf_op jit(solution)/shard_map/ppermute | solution.py:37
  219.5 31.6 %collective-permute-start.2 = (f32[128,128]{1,0:T(8,128)S(1)}, f32[128,128]{1,0:T(8,128)S(1)}, u32[]{:S(2)}, u32[]{:S(2)}) collective-permute-start(f32[128,128]{1,0:T(8,128)S(1)} %get-tuple-element.38), channel_id=1, source_target_pairs={{0,4},{4,8},{8,12},{12,16},{16,20},{20,24},{24,28},{28,32},{32,36}... | collective-permute-start | bytes 196616 | tf_op jit(solution)/shard_map/ppermute | solution.py:37
  221.5 29.6 %collective-permute-start.3 = (f32[128,128]{1,0:T(8,128)S(1)}, f32[128,128]{1,0:T(8,128)S(1)}, u32[]{:S(2)}, u32[]{:S(2)}) collective-permute-start(f32[128,128]{1,0:T(8,128)S(1)} %get-tuple-element.38), channel_id=1, source_target_pairs={{0,508},{4,0},{8,4},{12,8},{16,12},{20,16},{24,20},{28,24},{32,28}... | collective-permute-start | bytes 196616 | tf_op jit(solution)/shard_map/ppermute | solution.py:37
  235.7 15.5 %collective-permute-start.4 = (f32[128,128]{1,0:T(8,128)S(1)}, f32[128,128]{1,0:T(8,128)S(1)}, u32[]{:S(2)}, u32[]{:S(2)}) collective-permute-start(f32[128,128]{1,0:T(8,128)S(1)} %get-tuple-element.38), channel_id=1, source_target_pairs={{0,8},{4,12},{8,16},{12,20},{16,24},{20,28},{24,32},{28,36},{32,40... | collective-permute-start | bytes 196616 | tf_op jit(solution)/shard_map/ppermute | solution.py:37
  237.7 14.6 %collective-permute-start.5 = (f32[128,128]{1,0:T(8,128)S(1)}, f32[128,128]{1,0:T(8,128)S(1)}, u32[]{:S(2)}, u32[]{:S(2)}) collective-permute-start(f32[128,128]{1,0:T(8,128)S(1)} %get-tuple-element.38), channel_id=1, source_target_pairs={{0,504},{4,508},{8,0},{12,4},{16,8},{20,12},{24,16},{28,20},{32,24... | collective-permute-start | bytes 196616 | tf_op jit(solution)/shard_map/ppermute | solution.py:37
  254.8 37.2 %all-to-all-start.1 = ((f32[4,1,33024]{2,1,0:T(1,128)}), f32[4,1,33024]{2,1,0:T(1,128)S(1)}, u32[]{:S(2)}, u32[]{:S(2)}) async-start(f32[4,1,33024]{2,1,0:T(1,128)} %broadcast_in_dim.31), calls=%async_computation.1 | async-start | bytes 1056768 | tf_op jit(solution)/shard_map/all_to_all | solution.py:42
  292.4 6.1 %copy-start.1 = (f32[33024]{0:T(1024)}, f32[33024]{0:T(1024)S(1)}, u32[]{:S(2)}) copy-start(f32[33024]{0:T(1024)S(1)} %reduce_sum.39) | copy-start | bytes 396292
  299.1 0.7 slice-start
where the time goes:
time: 344 us; the launch traced here: 343 us
  starting transfers between devices  179 us (52%)
  waiting for transfers between devices  80.5 us (23%)
  blocking collectives  40.8 us (12%)
  local copies, waits for them, and re-layouts  20.2 us (6%)
  other arithmetic  12.4 us (4%)
  matrix products  8.87 us (3%)
    ppermute x8, starting transfers between devices, passed_along(): return lax.ppermute(value, axis, pairs)  62.6 us
    all_to_all x1, starting transfers between devices, local(): lax.all_to_all(predicted_grid, 'mem', split_axis=2, concat_axis=0, tiled=...  47.4 us
    all_to_all x1, blocking collectives, local(): lax.all_to_all(apply_weights(zone_collection, mixing), 'mem', split_axis=...  40.8 us
    ppermute x3, starting transfers between devices, padded_2(): lax.ppermute(tail, axis, [(i, (i + 1) % count) for i in range(count)])  31.3 us
    all_to_all x1, waiting for transfers between devices, local(): lax.all_to_all(predicted_grid, 'mem', split_axis=2, concat_axis=0, tiled=...  23.9 us
    ppermute x3, waiting for transfers between devices, padded_2(): lax.ppermute(head, axis, [((i + 1) % count, i) for i in range(count)])  20.7 us
    all_to_all x1, starting transfers between devices, sent_to_all(): lax.all_to_all(jnp.broadcast_to(value[None], (size, *value.shape)), axis,...  20.6 us
    ppermute x3, waiting for transfers between devices, padded_2(): lax.ppermute(tail, axis, [(i, (i + 1) % count) for i in range(count)])  18.3 us
  transfers between devices with their start and end apart: 16, of which 7 were waited for; matrix products, arithmetic and copies ran while one was open for 0% of the time, Pallas kernels for 0%

commit v1 on v0

--- a/solution.py
+++ b/solution.py
@@ -198,9 +198,10 @@
     )
     gram_matrix, pull_vector = together((gram_matrix, pull_vector), "slab")
     mixing = weights_from(gram_matrix, pull_vector, members)
-    return lax.all_to_all(
-        apply_weights(zone_collection, mixing), "mem", split_axis=0, concat_axis=2, tiled=True
-    )
+    change_members_all = lambda page: jnp.concatenate(
+        lax.all_to_all(jnp.stack(jnp.split(page, lax.psum(1, "mem"), 0), 0), "mem", 0, 0), 2
+    )
+    return change_members_all(apply_weights(zone_collection, mixing))
 
 
 def solution(mesh):

time: 344 us -> 346 us (level)
  no operation moved by 1% of the time
where the time goes in v1:
time: 346 us; the launch traced here: 345 us
  starting transfers between devices  179 us (52%)
  waiting for transfers between devices  80.3 us (23%)
  blocking collectives  40.8 us (12%)
  local copies, waits for them, and re-layouts  21.6 us (6%)
  other arithmetic  12.5 us (4%)
  matrix products  8.87 us (3%)
    ppermute x8, starting transfers between devices, passed_along(): return lax.ppermute(value, axis, pairs)  62.6 us
    all_to_all x1, starting transfers between devices, local(): lax.all_to_all(predicted_grid, 'mem', split_axis=2, concat_axis=0, tiled=...  47.4 us
    all_to_all x1, blocking collectives, local(): lax.all_to_all(jnp.stack(jnp.split(page, lax.psum(1, 'mem'), 0), 0), 'mem...  40.8 us
    ppermute x3, starting transfers between devices, padded_2(): lax.ppermute(tail, axis, [(i, (i + 1) % count) for i in range(count)])  31.3 us
    all_to_all x1, waiting for transfers between devices, local(): lax.all_to_all(predicted_grid, 'mem', split_axis=2, concat_axis=0, tiled=...  23.9 us
    ppermute x3, waiting for transfers between devices, padded_2(): lax.ppermute(head, axis, [((i + 1) % count, i) for i in range(count)])  20.7 us
    all_to_all x1, starting transfers between devices, sent_to_all(): lax.all_to_all(jnp.broadcast_to(value[None], (size, *value.shape)), axis,...  20.6 us
    ppermute x3, waiting for transfers between devices, padded_2(): lax.ppermute(tail, axis, [(i, (i + 1) % count) for i in range(count)])  18.3 us
  transfers between devices with their start and end apart: 16, of which 7 were waited for; matrix products, arithmetic and copies ran while one was open for 0% of the time, Pallas kernels for 0%

profile of v1, /device:TPU:1, one launch (start us, length us, event | category | flops | bytes accessed | tf_op | source)
XLA Modules:
  0.0 345.1 jit_solution(12778864894171161533)
XLA Ops:
  0.0 1.0 copy-done
  1.0 111.7 %while.10 = (s32[]{:T(128)}, f32[3,256,128]{2,1,0:T(8,128)S(1)}, s32[]{:T(128)}) while((s32[]{:T(128)}, f32[3,256,128]{2,1,0:T(8,128)S(1)}, s32[]{:T(128)}) %tuple.295), condition=%wide.region_1.2_spmd, body=%wide.region_0.1_spmd.sunk | while | flops 9566210 | bytes 27316348 | solution.py:169
  1.2 8.7 %collective-permute-start = (f32[3,256,4]{2,1,0:T(8,128)S(1)}, f32[3,256,4]{2,1,0:T(8,128)S(1)}, u32[]{:S(2)}, u32[]{:S(2)}) collective-permute-start(f32[3,256,4]{2,1,0:T(8,128)S(1)} %get-tuple-element.391), channel_id=1, source_target_pairs={{1,0},{2,1},{3,2},{0,3},{5,4},{6,5},{7,6},{4,7},{9,8},{10,9},{11,1... | collective-permute-start | bytes 36872 | tf_op jit(solution)/shard_map/while/body/eval_jaxpr/ppermute | solution.py:27
  9.9 10.0 %collective-permute-start.1 = (f32[3,256,4]{2,1,0:T(8,128)S(1)}, f32[3,256,4]{2,1,0:T(8,128)S(1)}, u32[]{:S(2)}, u32[]{:S(2)}) collective-permute-start(f32[3,256,4]{2,1,0:T(8,128)S(1)} %get-tuple-element.392), channel_id=1, source_target_pairs={{0,1},{1,2},{2,3},{3,0},{4,5},{5,6},{6,7},{7,4},{8,9},{9,10},{10,1... | collective-permute-start | bytes 36872 | tf_op jit(solution)/shard_map/while/body/eval_jaxpr/ppermute | solution.py:25
  19.9 3.8 %collective-permute-done = f32[3,256,4]{2,1,0:T(8,128)S(1)} collective-permute-done((f32[3,256,4]{2,1,0:T(8,128)S(1)}, f32[3,256,4]{2,1,0:T(8,128)S(1)}, u32[]{:S(2)}, u32[]{:S(2)}) %collective-permute-start) | collective-permute-done | bytes 12320 | tf_op jit(solution)/shard_map/while/body/eval_jaxpr/ppermute | solution.py:27
  23.7 18.3 %collective-permute-done.1 = f32[3,256,4]{2,1,0:T(8,128)S(1)} collective-permute-done((f32[3,256,4]{2,1,0:T(8,128)S(1)}, f32[3,256,4]{2,1,0:T(8,128)S(1)}, u32[]{:S(2)}, u32[]{:S(2)}) %collective-permute-start.1) | collective-permute-done | bytes 12320 | tf_op jit(solution)/shard_map/while/body/eval_jaxpr/ppermute | solution.py:25
  42.0 0.4 pad_maximum_fusion.30
  42.5 0.3 fusion.199
  43.0 0.3 fusion.197
  43.4 0.6 add_multiply_fusion.16
  44.8 0.3 add_multiply_fusion.17
  45.4 0.6 add_multiply_fusion.18
  46.8 0.3 add_multiply_fusion.19
  47.5 0.6 add_multiply_fusion.20
  48.7 0.3 add_multiply_fusion.21
  50.1 3.3 collective-permute-start
  53.4 11.9 %collective-permute-start.1 = (f32[3,256,4]{2,1,0:T(8,128)S(1)}, f32[3,256,4]{2,1,0:T(8,128)S(1)}, u32[]{:S(2)}, u32[]{:S(2)}) collective-permute-start(f32[3,256,4]{2,1,0:T(8,128)S(1)} %get-tuple-element.392), channel_id=1, source_target_pairs={{0,1},{1,2},{2,3},{3,0},{4,5},{5,6},{6,7},{7,4},{8,9},{9,10},{10,1... | collective-permute-start | bytes 36872 | tf_op jit(solution)/shard_map/while/body/eval_jaxpr/ppermute | solution.py:25
  65.4 11.8 %collective-permute-done = f32[3,256,4]{2,1,0:T(8,128)S(1)} collective-permute-done((f32[3,256,4]{2,1,0:T(8,128)S(1)}, f32[3,256,4]{2,1,0:T(8,128)S(1)}, u32[]{:S(2)}, u32[]{:S(2)}) %collective-permute-start) | collective-permute-done | bytes 12320 | tf_op jit(solution)/shard_map/while/body/eval_jaxpr/ppermute | solution.py:27
  77.1 0.4 pad_maximum_fusion.30
  77.6 0.3 fusion.199
  78.1 0.3 fusion.197
  78.5 0.6 add_multiply_fusion.16
  79.9 0.3 add_multiply_fusion.17
  80.5 0.6 add_multiply_fusion.18
  81.9 0.3 add_multiply_fusion.19
  82.6 0.6 add_multiply_fusion.20
  83.8 0.3 add_multiply_fusion.21
  85.2 5.1 %collective-permute-start = (f32[3,256,4]{2,1,0:T(8,128)S(1)}, f32[3,256,4]{2,1,0:T(8,128)S(1)}, u32[]{:S(2)}, u32[]{:S(2)}) collective-permute-start(f32[3,256,4]{2,1,0:T(8,128)S(1)} %get-tuple-element.391), channel_id=1, source_target_pairs={{1,0},{2,1},{3,2},{0,3},{5,4},{6,5},{7,6},{4,7},{9,8},{10,9},{11,1... | collective-permute-start | bytes 36872 | tf_op jit(solution)/shard_map/while/body/eval_jaxpr/ppermute | solution.py:27
  90.3 9.4 %collective-permute-start.1 = (f32[3,256,4]{2,1,0:T(8,128)S(1)}, f32[3,256,4]{2,1,0:T(8,128)S(1)}, u32[]{:S(2)}, u32[]{:S(2)}) collective-permute-start(f32[3,256,4]{2,1,0:T(8,128)S(1)} %get-tuple-element.392), channel_id=1, source_target_pairs={{0,1},{1,2},{2,3},{3,0},{4,5},{5,6},{6,7},{7,4},{8,9},{9,10},{10,1... | collective-permute-start | bytes 36872 | tf_op jit(solution)/shard_map/while/body/eval_jaxpr/ppermute | solution.py:25
  99.7 5.1 %collective-permute-done = f32[3,256,4]{2,1,0:T(8,128)S(1)} collective-permute-done((f32[3,256,4]{2,1,0:T(8,128)S(1)}, f32[3,256,4]{2,1,0:T(8,128)S(1)}, u32[]{:S(2)}, u32[]{:S(2)}) %collective-permute-start) | collective-permute-done | bytes 12320 | tf_op jit(solution)/shard_map/while/body/eval_jaxpr/ppermute | solution.py:27
  104.8 0.4 pad_maximum_fusion.30
  105.4 0.3 fusion.199
  106.2 0.6 add_multiply_fusion.16
  107.6 0.3 add_multiply_fusion.17
  108.2 0.6 add_multiply_fusion.18
  109.7 0.3 add_multiply_fusion.19
  110.3 0.6 add_multiply_fusion.20
  111.5 0.3 add_multiply_fusion.21
  112.7 1.2 copy.4843
  113.9 47.4 %all-to-all-start = ((f32[1,3,256,128]{3,0,1,2:T(1,128)}), f32[1,3,256,128]{3,0,1,2:T(1,128)S(1)}, u32[]{:S(2)}, u32[]{:S(2)}) async-start(f32[1,3,256,128]{3,0,1,2:T(1,128)} %copy.4843), calls=%async_computation | async-start | bytes 786432 | tf_op jit(solution)/shard_map/all_to_all | solution.py:171
  161.3 0.6 copy-done.3
  162.0 0.6 copy-done.4
  162.6 23.9 %all-to-all-done = f32[1,3,256,128]{3,0,1,2:T(1,128)S(1)} async-done(((f32[1,3,256,128]{3,0,1,2:T(1,128)}), f32[1,3,256,128]{3,0,1,2:T(1,128)S(1)}, u32[]{:S(2)}, u32[]{:S(2)}) %all-to-all-start) | async-done | bytes 393248 | tf_op jit(solution)/shard_map/all_to_all | solution.py:171
  186.7 0.6 gather_fusion
  187.5 0.6 copy-done.2
  188.2 2.6 collective-permute-start.6
  190.8 13.5 %collective-permute-start.7 = (f32[3,128]{1,0:T(4,128)S(1)}, f32[3,128]{1,0:T(4,128)S(1)}, u32[]{:S(2)}, u32[]{:S(2)}) collective-permute-start(f32[3,128]{1,0:T(4,128)S(1)} %pad_maximum_fusion.27), channel_id=1, source_target_pairs={{0,508},{4,0},{8,4},{12,8},{16,12},{20,16},{24,20},{28,24},{32,28}... | collective-permute-start | bytes 4616 | tf_op jit(solution)/shard_map/ppermute | solution.py:37
  204.3 1.9 collective-permute-start.8
  206.2 13.3 %collective-permute-start.9 = (f32[3,128]{1,0:T(4,128)S(1)}, f32[3,128]{1,0:T(4,128)S(1)}, u32[]{:S(2)}, u32[]{:S(2)}) collective-permute-start(f32[3,128]{1,0:T(4,128)S(1)} %pad_maximum_fusion.27), channel_id=1, source_target_pairs={{0,504},{4,508},{8,0},{12,4},{16,8},{20,12},{24,16},{28,20},{32,24... | collective-permute-start | bytes 4616 | tf_op jit(solution)/shard_map/ppermute | solution.py:37
  219.5 1.9 collective-permute-start.2
  221.5 14.2 %collective-permute-start.3 = (f32[128,128]{1,0:T(8,128)S(1)}, f32[128,128]{1,0:T(8,128)S(1)}, u32[]{:S(2)}, u32[]{:S(2)}) collective-permute-start(f32[128,128]{1,0:T(8,128)S(1)} %get-tuple-element.38), channel_id=1, source_target_pairs={{0,508},{4,0},{8,4},{12,8},{16,12},{20,16},{24,20},{28,24},{32,28}... | collective-permute-start | bytes 196616 | tf_op jit(solution)/shard_map/ppermute | solution.py:37
  235.7 1.9 collective-permute-start.4
  237.7 13.3 %collective-permute-start.5 = (f32[128,128]{1,0:T(8,128)S(1)}, f32[128,128]{1,0:T(8,128)S(1)}, u32[]{:S(2)}, u32[]{:S(2)}) collective-permute-start(f32[128,128]{1,0:T(8,128)S(1)} %get-tuple-element.38), channel_id=1, source_target_pairs={{0,504},{4,508},{8,0},{12,4},{16,8},{20,12},{24,16},{28,20},{32,24... | collective-permute-start | bytes 196616 | tf_op jit(solution)/shard_map/ppermute | solution.py:37
  251.2 1.1 collective-permute-done.5
  252.3 0.7 fusion.36
  253.0 0.6 fusion.34
  253.7 1.1 broadcast_in_dim.31
  254.8 20.6 %all-to-all-start.1 = ((f32[4,1,33024]{2,1,0:T(1,128)}), f32[4,1,33024]{2,1,0:T(1,128)S(1)}, u32[]{:S(2)}, u32[]{:S(2)}) async-start(f32[4,1,33024]{2,1,0:T(1,128)} %broadcast_in_dim.31), calls=%async_computation.1 | async-start | bytes 1056768 | tf_op jit(solution)/shard_map/all_to_all | solution.py:42
  275.6 16.4 %all-to-all-done.1 = f32[4,1,33024]{2,1,0:T(1,128)S(1)} async-done(((f32[4,1,33024]{2,1,0:T(1,128)}), f32[4,1,33024]{2,1,0:T(1,128)S(1)}, u32[]{:S(2)}, u32[]{:S(2)}) %all-to-all-start.1) | async-done | bytes 528416 | tf_op jit(solution)/shard_map/all_to_all | solution.py:42
  292.0 0.5 reduce_sum.39
  299.1 0.7 slice-done
  300.4 0.6 fusion.25
  303.4 40.8 %all_to_all.29 = f32[128,1,3,2,128]{4,3,2,1,0:T(2,128)S(1)} all-to-all(f32[128,1,3,2,128]{4,3,2,1,0:T(2,128)S(1)} %copy.4913), channel_id=1, replica_groups=mesh['mem'=128,'slab'=4] {'mem'}, dimensions={0} | all-to-all | bytes 786432 | tf_op jit(solution)/shard_map/all_to_all | solution.py:202
  344.3 0.8 copy.4915
  (335 shorter events, 22.3 us)
Async XLA Ops:
  0.0 1.0 copy-start
  1.2 22.6 %collective-permute-start = (f32[3,256,4]{2,1,0:T(8,128)S(1)}, f32[3,256,4]{2,1,0:T(8,128)S(1)}, u32[]{:S(2)}, u32[]{:S(2)}) collective-permute-start(f32[3,256,4]{2,1,0:T(8,128)S(1)} %get-tuple-element.391), channel_id=1, source_target_pairs={{1,0},{2,1},{3,2},{0,3},{5,4},{6,5},{7,6},{4,7},{9,8},{10,9},{11,1... | collective-permute-start | bytes 36872 | tf_op jit(solution)/shard_map/while/body/eval_jaxpr/ppermute | solution.py:27
  9.9 32.1 %collective-permute-start.1 = (f32[3,256,4]{2,1,0:T(8,128)S(1)}, f32[3,256,4]{2,1,0:T(8,128)S(1)}, u32[]{:S(2)}, u32[]{:S(2)}) collective-permute-start(f32[3,256,4]{2,1,0:T(8,128)S(1)} %get-tuple-element.392), channel_id=1, source_target_pairs={{0,1},{1,2},{2,3},{3,0},{4,5},{5,6},{6,7},{7,4},{8,9},{9,10},{10,1... | collective-permute-start | bytes 36872 | tf_op jit(solution)/shard_map/while/body/eval_jaxpr/ppermute | solution.py:25
  50.1 27.0 %collective-permute-start = (f32[3,256,4]{2,1,0:T(8,128)S(1)}, f32[3,256,4]{2,1,0:T(8,128)S(1)}, u32[]{:S(2)}, u32[]{:S(2)}) collective-permute-start(f32[3,256,4]{2,1,0:T(8,128)S(1)} %get-tuple-element.391), channel_id=1, source_target_pairs={{1,0},{2,1},{3,2},{0,3},{5,4},{6,5},{7,6},{4,7},{9,8},{10,9},{11,1... | collective-permute-start | bytes 36872 | tf_op jit(solution)/shard_map/while/body/eval_jaxpr/ppermute | solution.py:27
  53.4 23.7 %collective-permute-start.1 = (f32[3,256,4]{2,1,0:T(8,128)S(1)}, f32[3,256,4]{2,1,0:T(8,128)S(1)}, u32[]{:S(2)}, u32[]{:S(2)}) collective-permute-start(f32[3,256,4]{2,1,0:T(8,128)S(1)} %get-tuple-element.392), channel_id=1, source_target_pairs={{0,1},{1,2},{2,3},{3,0},{4,5},{5,6},{6,7},{7,4},{8,9},{9,10},{10,1... | collective-permute-start | bytes 36872 | tf_op jit(solution)/shard_map/while/body/eval_jaxpr/ppermute | solution.py:25
  85.2 19.6 %collective-permute-start = (f32[3,256,4]{2,1,0:T(8,128)S(1)}, f32[3,256,4]{2,1,0:T(8,128)S(1)}, u32[]{:S(2)}, u32[]{:S(2)}) collective-permute-start(f32[3,256,4]{2,1,0:T(8,128)S(1)} %get-tuple-element.391), channel_id=1, source_target_pairs={{1,0},{2,1},{3,2},{0,3},{5,4},{6,5},{7,6},{4,7},{9,8},{10,9},{11,1... | collective-permute-start | bytes 36872 | tf_op jit(solution)/shard_map/while/body/eval_jaxpr/ppermute | solution.py:27
  90.3 14.5 %collective-permute-start.1 = (f32[3,256,4]{2,1,0:T(8,128)S(1)}, f32[3,256,4]{2,1,0:T(8,128)S(1)}, u32[]{:S(2)}, u32[]{:S(2)}) collective-permute-start(f32[3,256,4]{2,1,0:T(8,128)S(1)} %get-tuple-element.392), channel_id=1, source_target_pairs={{0,1},{1,2},{2,3},{3,0},{4,5},{5,6},{6,7},{7,4},{8,9},{9,10},{10,1... | collective-permute-start | bytes 36872 | tf_op jit(solution)/shard_map/while/body/eval_jaxpr/ppermute | solution.py:25
  113.9 72.7 %all-to-all-start = ((f32[1,3,256,128]{3,0,1,2:T(1,128)}), f32[1,3,256,128]{3,0,1,2:T(1,128)S(1)}, u32[]{:S(2)}, u32[]{:S(2)}) async-start(f32[1,3,256,128]{3,0,1,2:T(1,128)} %copy.4843), calls=%async_computation | async-start | bytes 786432 | tf_op jit(solution)/shard_map/all_to_all | solution.py:171
  161.3 0.7 copy-start.3
  162.0 0.7 copy-start.4
  187.5 0.7 copy-start.2
  188.2 33.3 %collective-permute-start.6 = (f32[3,128]{1,0:T(4,128)S(1)}, f32[3,128]{1,0:T(4,128)S(1)}, u32[]{:S(2)}, u32[]{:S(2)}) collective-permute-start(f32[3,128]{1,0:T(4,128)S(1)} %pad_maximum_fusion.27), channel_id=1, source_target_pairs={{0,4},{4,8},{8,12},{12,16},{16,20},{20,24},{24,28},{28,32},{32,36}... | collective-permute-start | bytes 4616 | tf_op jit(solution)/shard_map/ppermute | solution.py:37
  190.8 44.9 %collective-permute-start.7 = (f32[3,128]{1,0:T(4,128)S(1)}, f32[3,128]{1,0:T(4,128)S(1)}, u32[]{:S(2)}, u32[]{:S(2)}) collective-permute-start(f32[3,128]{1,0:T(4,128)S(1)} %pad_maximum_fusion.27), channel_id=1, source_target_pairs={{0,508},{4,0},{8,4},{12,8},{16,12},{20,16},{24,20},{28,24},{32,28}... | collective-permute-start | bytes 4616 | tf_op jit(solution)/shard_map/ppermute | solution.py:37
  204.3 33.4 %collective-permute-start.8 = (f32[3,128]{1,0:T(4,128)S(1)}, f32[3,128]{1,0:T(4,128)S(1)}, u32[]{:S(2)}, u32[]{:S(2)}) collective-permute-start(f32[3,128]{1,0:T(4,128)S(1)} %pad_maximum_fusion.27), channel_id=1, source_target_pairs={{0,8},{4,12},{8,16},{12,20},{16,24},{20,28},{24,32},{28,36},{32,40... | collective-permute-start | bytes 4616 | tf_op jit(solution)/shard_map/ppermute | solution.py:37
  206.2 44.8 %collective-permute-start.9 = (f32[3,128]{1,0:T(4,128)S(1)}, f32[3,128]{1,0:T(4,128)S(1)}, u32[]{:S(2)}, u32[]{:S(2)}) collective-permute-start(f32[3,128]{1,0:T(4,128)S(1)} %pad_maximum_fusion.27), channel_id=1, source_target_pairs={{0,504},{4,508},{8,0},{12,4},{16,8},{20,12},{24,16},{28,20},{32,24... | collective-permute-start | bytes 4616 | tf_op jit(solution)/shard_map/ppermute | solution.py:37
  219.5 31.6 %collective-permute-start.2 = (f32[128,128]{1,0:T(8,128)S(1)}, f32[128,128]{1,0:T(8,128)S(1)}, u32[]{:S(2)}, u32[]{:S(2)}) collective-permute-start(f32[128,128]{1,0:T(8,128)S(1)} %get-tuple-element.38), channel_id=1, source_target_pairs={{0,4},{4,8},{8,12},{12,16},{16,20},{20,24},{24,28},{28,32},{32,36}... | collective-permute-start | bytes 196616 | tf_op jit(solution)/shard_map/ppermute | solution.py:37
  221.5 29.6 %collective-permute-start.3 = (f32[128,128]{1,0:T(8,128)S(1)}, f32[128,128]{1,0:T(8,128)S(1)}, u32[]{:S(2)}, u32[]{:S(2)}) collective-permute-start(f32[128,128]{1,0:T(8,128)S(1)} %get-tuple-element.38), channel_id=1, source_target_pairs={{0,508},{4,0},{8,4},{12,8},{16,12},{20,16},{24,20},{28,24},{32,28}... | collective-permute-start | bytes 196616 | tf_op jit(solution)/shard_map/ppermute | solution.py:37
  235.7 15.5 %collective-permute-start.4 = (f32[128,128]{1,0:T(8,128)S(1)}, f32[128,128]{1,0:T(8,128)S(1)}, u32[]{:S(2)}, u32[]{:S(2)}) collective-permute-start(f32[128,128]{1,0:T(8,128)S(1)} %get-tuple-element.38), channel_id=1, source_target_pairs={{0,8},{4,12},{8,16},{12,20},{16,24},{20,28},{24,32},{28,36},{32,40... | collective-permute-start | bytes 196616 | tf_op jit(solution)/shard_map/ppermute | solution.py:37
  237.7 14.6 %collective-permute-start.5 = (f32[128,128]{1,0:T(8,128)S(1)}, f32[128,128]{1,0:T(8,128)S(1)}, u32[]{:S(2)}, u32[]{:S(2)}) collective-permute-start(f32[128,128]{1,0:T(8,128)S(1)} %get-tuple-element.38), channel_id=1, source_target_pairs={{0,504},{4,508},{8,0},{12,4},{16,8},{20,12},{24,16},{28,20},{32,24... | collective-permute-start | bytes 196616 | tf_op jit(solution)/shard_map/ppermute | solution.py:37
  254.8 37.2 %all-to-all-start.1 = ((f32[4,1,33024]{2,1,0:T(1,128)}), f32[4,1,33024]{2,1,0:T(1,128)S(1)}, u32[]{:S(2)}, u32[]{:S(2)}) async-start(f32[4,1,33024]{2,1,0:T(1,128)} %broadcast_in_dim.31), calls=%async_computation.1 | async-start | bytes 1056768 | tf_op jit(solution)/shard_map/all_to_all | solution.py:42
  292.5 6.1 %copy-start.1 = (f32[33024]{0:T(1024)}, f32[33024]{0:T(1024)S(1)}, u32[]{:S(2)}) copy-start(f32[33024]{0:T(1024)S(1)} %reduce_sum.39) | copy-start | bytes 396292
  299.1 0.7 slice-start
